TPU v7x, 32 devices: a whole 2x2x4 slice. The times are simulated.
32 devices in a mesh: seq: 4 (over y, x), mem: 8 (over z, core).
Axes of the slice: x: 2, y: 2, z: 4, core: 2. Of those that a mesh axis runs over, the one named last changes fastest.
Arguments:
- hidden: bfloat16 [8192, 2048], P(('seq', 'mem')), may hold values from -6 to 6
- routes: int32 [8192, 2], P(('seq', 'mem')), may hold values from 0 to 7, all different within a row; in each aligned block of 256 rows (0 to 255, 256 to 511, ...) at most 64 rows name the same one
- gate_levels: int32 [8192, 2], P(('seq', 'mem')), may hold values from 1 to 255
- query_weight: bfloat16 [2048, 1024], P('seq'), may hold values from -0.125 to 0.125
- key_weight: bfloat16 [8, 2048, 1024], P('mem', 'seq'), may hold values from -0.125 to 0.125
- value_weight: bfloat16 [8, 2048, 1024], P('mem', 'seq'), may hold values from -0.125 to 0.125
Outputs:
- mixed: bfloat16 [8192, 1024], P(('seq', 'mem'))
Inputs may be any that keep to these rules, and one draw needn't show every extreme that they name: `routes`: the two memories of a row differ. In the rows of one device no memory is named by more than 64 rows, a bound that some block reaches.
All inputs are finite; a program needn't handle non-finite values.
Results may differ from a plain program's by a relative error of at most 0.01.
Values may be sent and summed in bfloat16 or wider, within the bound.
No kernel may reach another device: no remote copies, remote signals or barrier semaphores. Data moves between devices by JAX's collectives and lax.ppermute only.
A program may use at most 128 MiB of HBM per device.

v0:
```python
import jax
import jax.numpy as jnp
from jax import lax
from jax.sharding import PartitionSpec as P

HEADS = 8
DK = 128
BLOCK = 512
CAP = 64


def entering(array, axis, join, neutral):
    place = lax.axis_index(axis)
    gathered = lax.all_gather(array.astype(jnp.bfloat16), axis)
    state = jnp.zeros_like(array) + jnp.asarray(neutral, array.dtype)

    def one(step, state):
        return join(state, lax.dynamic_index_in_dim(gathered, step, 0, False).astype(array.dtype))

    return lax.fori_loop(0, place, one, state)


def add_states(earlier, later):
    return earlier + later


def on_device(hidden, routes, gate_levels, query_weight, key_weight, value_weight):
    count = hidden.shape[0]
    model = hidden.shape[1]
    width = query_weight.shape[1]
    mem_local = key_weight.shape[0]
    experts = mem_local * lax.axis_size("mem")
    highest = lax.Precision.HIGHEST
    onehot = (routes[:, :, None] == jnp.arange(experts, dtype=jnp.int32)[None, None, :]).astype(
        jnp.int32
    )
    per_token = jnp.sum(onehot, axis=1)
    before = jnp.cumsum(per_token, axis=0) - per_token
    place = jnp.sum(onehot * before[:, None, :], axis=2)
    slots = (routes * CAP + place).reshape(-1)
    owner_of = jnp.arange(2 * count, dtype=jnp.int32) // 2
    match = jnp.arange(experts * CAP, dtype=jnp.int32)[:, None] == slots[None, :]
    source = jnp.sum(jnp.where(match, owner_of[None, :], 0), axis=1)
    filled = jnp.any(match, axis=1)
    sent_rows = jnp.where(
        filled[:, None], jnp.take(hidden, source, axis=0), jnp.zeros((), hidden.dtype)
    )
    sent_rows = sent_rows.reshape(experts, CAP, model)
    columns = hidden
    queries = jnp.dot(
        columns,
        lax.all_gather(query_weight, "seq", axis=0, tiled=True),
        preferred_element_type=jnp.float32,
    ).astype(jnp.bfloat16)
    sent_queries = jnp.where(
        filled[:, None], jnp.take(queries, source, axis=0), jnp.zeros((), queries.dtype)
    )
    sent_queries = sent_queries.reshape(experts, CAP, width)
    arrived, arrived_queries = (
        lax.all_to_all(sent_rows, "mem", split_axis=0, concat_axis=1, tiled=True),
        lax.all_to_all(sent_queries, "mem", split_axis=0, concat_axis=1, tiled=True),
    )
    length = arrived.shape[1]
    columns = arrived
    key_part = jnp.einsum(
        "mrc,mch->mrh",
        columns,
        lax.all_gather(key_weight, "seq", axis=1, tiled=True),
        preferred_element_type=jnp.float32,
    )
    value_part = jnp.einsum(
        "mrc,mch->mrh",
        columns,
        lax.all_gather(value_weight, "seq", axis=1, tiled=True),
        preferred_element_type=jnp.float32,
    )
    keys = key_part
    values = value_part
    keys = keys.astype(jnp.bfloat16)
    values = values.astype(jnp.bfloat16)
    nblocks = length // BLOCK
    shape5 = (mem_local, nblocks, BLOCK, HEADS, DK)
    q_five = arrived_queries.reshape(shape5)
    k_five = keys.reshape(shape5)
    v_five = values.reshape(shape5)
    block_states = jnp.einsum(
        "mnkhd,mnkhe->mnhde", k_five, v_five, preferred_element_type=jnp.float32
    )
    within = jnp.cumsum(block_states, axis=1) - block_states
    local_total = jnp.sum(block_states, axis=1)
    nothing = jnp.zeros_like(local_total)
    incoming = entering(local_total, "seq", add_states, nothing)
    states = (incoming[:, None] + within).reshape(mem_local * nblocks, HEADS, DK, DK)
    flat = (mem_local * nblocks, BLOCK, HEADS, DK)
    rowids = jnp.arange(BLOCK, dtype=jnp.int32)
    causal = (rowids[:, None] >= rowids[None, :]).astype(jnp.float32)

    def attend(inputs):
        q_block, k_block, v_block, state = inputs
        scores = (
            jnp.einsum("qhd,khd->hqk", q_block, k_block, preferred_element_type=jnp.float32)
            * causal[None]
        )
        local = jnp.einsum("hqk,khd->qhd", scores, v_block.astype(jnp.float32), precision=highest)
        carried = jnp.einsum("qhd,hde->qhe", q_block.astype(jnp.float32), state, precision=highest)
        reads = local + carried
        scale = lax.rsqrt(jnp.mean(reads * reads, axis=-1, keepdims=True) + 1e-06)
        return (reads * scale).astype(jnp.bfloat16)

    normed = lax.map(
        attend, (q_five.reshape(flat), k_five.reshape(flat), v_five.reshape(flat), states)
    )
    normed = normed.reshape(mem_local, length, width)
    returned = lax.all_to_all(normed, "mem", split_axis=1, concat_axis=0, tiled=True)
    returned = returned.reshape(experts * CAP, width)
    picked = jnp.take(returned, slots, axis=0).reshape(count, 2, width)
    levels = gate_levels.astype(jnp.float32)
    gates = levels / jnp.sum(levels, axis=1, keepdims=True)
    mixed = jnp.sum(gates[:, :, None] * picked.astype(jnp.float32), axis=1)
    return mixed.astype(jnp.bfloat16)


def solution(mesh):
    return jax.shard_map(
        on_device,
        mesh=mesh,
        in_specs=(
            P(("seq", "mem"), None),
            P(("seq", "mem"), None),
            P(("seq", "mem"), None),
            P("seq", None),
            P("mem", "seq", None),
            P("mem", "seq", None),
        ),
        out_specs=P(("seq", "mem"), None),
        check_vma=False,
    )
```

profile of v0, /device:TPU:0, one launch (start us, length us, event | category | flops | bytes accessed | tf_op | source)
XLA Modules:
  0.0 289.7 jit_solution(13704537950358973058)
XLA Ops:
  6.5 0.0 copy-start
  6.5 0.0 all-gather.10.cloned.1.call-start
  6.5 0.7 all-gather.10.cloned.1.call-update
  7.3 0.0 all-gather.6.cloned.1.call-start
  7.3 0.7 all-gather.6.cloned.1.call-update
  8.0 0.0 all-gather.8.cloned.1.call-start
  8.1 0.7 all-gather.8.cloned.1.call-update
  8.7 0.0 all-gather.12.cloned.1.call-start
  8.8 0.0 copy-done.5
  8.8 0.6 reduce-window.6
  9.4 0.2 slice_reduce_fusion
  9.7 0.1 bitcast_subtract_fusion
  9.8 0.1 copy.61
  9.9 0.1 reshape.211
  10.1 0.2 fusion.24
  10.3 0.2 select_reduce_fusion
  10.5 0.1 reduce_sum.67
  10.5 0.1 broadcast_in_dim.94
  10.6 0.0 copy-done
  10.6 2.5 gather_fusion
  13.1 0.3 select_select_fusion
  13.5 55.2 %all_to_all.12 = bf16[8,64,2048]{2,1,0:T(8,128)(2,1)S(1)} all-to-all(bf16[8,64,2048]{2,1,0:T(8,128)(2,1)S(1)} %select_select_fusion), channel_id=1, replica_groups=mesh['seq'=4,'mem'=8] {'mem'}, dimensions={0} | all-to-all | bytes 4194304 | tf_op jit(solution)/shard_map/all_to_all | solution.py:60
  68.7 1.4 copy-done.4
  70.0 5.5 %fusion.15 = bf16[512,1024]{1,0:T(8,128)(2,1)} fusion(bf16[512,2048]{1,0:T(8,128)(2,1)S(1)} %bitcast.80, bf16[1,2048,1024]{2,1,0:T(8,128)(2,1)} %all-gather.10.cloned.1.call-done), kind=kOutput, calls=%fused_computation.20 | convolution fusion | flops 2148007936 | bytes 7340032 | tf_op jit(solution)/shard_map/mrc,mch->mrh/dot_general | solution.py:65
  75.5 1.6 copy.74
  77.1 41.9 %all-gather.6.cloned.1.call-done = bf16[1,2048,1024]{2,1,0:T(8,128)(2,1)} async-done(((bf16[1,512,1024]{2,1,0:T(8,128)(2,1)}), bf16[1,2048,1024]{2,1,0:T(8,128)(2,1)}) %all-gather.6.cloned.1.call-update) | async-done | bytes 4194320 | tf_op jit(solution)/shard_map/all_gather | solution.py:74
  119.0 5.2 %fusion.18 = bf16[64,8,8,128]{3,2,1,0:T(8,128)(2,1)S(1)} fusion(bf16[512,2048]{1,0:T(8,128)(2,1)} %bitcast.81, bf16[1,2048,1024]{2,1,0:T(8,128)(2,1)} %all-gather.6.cloned.1.call-done), kind=kOutput, calls=%fused_computation.21 | convolution fusion | flops 2148007936 | bytes 7340032 | tf_op jit(solution)/shard_map/mrc,mch->mrh/dot_general | solution.py:71
  124.2 0.0 copy-start.2
  124.2 1.0 copy-done.2
  125.2 1.2 fusion.36
  126.3 0.0 all-gather.12.cloned.1.call-update
  126.3 47.1 %all-gather.8.cloned.1.call-done = bf16[2048,1024]{1,0:T(8,128)(2,1)} async-done(((bf16[512,1024]{1,0:T(8,128)(2,1)}), bf16[2048,1024]{1,0:T(8,128)(2,1)}) %all-gather.8.cloned.1.call-update) | async-done | bytes 4194320 | tf_op jit(solution)/shard_map/all_gather | solution.py:52
  173.5 3.4 %convolution_convert_fusion = bf16[256,1024]{1,0:T(8,128)(2,1)S(1)} fusion(bf16[256,2048]{1,0:T(8,128)(2,1)S(1)} %copy-done, bf16[2048,1024]{1,0:T(8,128)(2,1)} %all-gather.8.cloned.1.call-done), kind=kOutput, calls=%fused_computation.22 | convolution fusion | flops 1074003968 | bytes 5767168 | tf_op jit(solution)/shard_map/dot_general | solution.py:50
  176.9 2.8 gather_fusion.1
  179.7 2.4 select_select_fusion.1
  182.1 4.6 %all-to-all-start.1 = ((bf16[8,64,1024]{2,1,0:T(8,128)(2,1)}), bf16[8,64,1024]{2,1,0:T(8,128)(2,1)}, u32[]{:S(2)}, u32[]{:S(2)}) async-start(bf16[8,64,1024]{2,1,0:T(8,128)(2,1)} %select_select_fusion.1), calls=%async_computation.1 | async-start | bytes 2097152 | tf_op jit(solution)/shard_map/all_to_all | solution.py:61
  186.7 1.1 fusion.25
  187.8 13.9 %all-gather.12.cloned.1.call-done = bf16[32,128,128]{2,1,0:T(8,128)(2,1)} async-done(((bf16[8,128,128]{2,1,0:T(8,128)(2,1)}), bf16[32,128,128]{2,1,0:T(8,128)(2,1)}) %all-gather.12.cloned.1.call-update) | async-done | bytes 1048592 | tf_op jit(solution)/shard_map/all_gather | solution.py:14
  201.7 0.2 while.2
  201.9 11.5 %all-to-all-done.1 = bf16[8,64,1024]{2,1,0:T(8,128)(2,1)} async-done(((bf16[8,64,1024]{2,1,0:T(8,128)(2,1)}), bf16[8,64,1024]{2,1,0:T(8,128)(2,1)}, u32[]{:S(2)}, u32[]{:S(2)}) %all-to-all-start.1) | async-done | bytes 1048608 | tf_op jit(solution)/shard_map/all_to_all | solution.py:61
  213.4 1.5 copy.76
  214.9 1.2 fusion.30
  216.1 0.0 copy-start.1
  216.2 0.0 copy-start.3
  216.2 1.1 fusion.28
  217.2 0.1 copy-done.1
  217.4 0.3 copy-done.3
  217.7 5.5 %fusion.7 = (f32[512,8]{0,1:T(8,128)S(1)}, f32[8,128,512]{2,1,0:T(8,128)S(1)}) fusion(f32[8,128,512]{2,1,0:T(8,128)S(1)} %fusion.28, f32[8,512,512]{2,1,0:T(8,128)S(1)} %fusion.30, f32[512,512]{1,0:T(8,128)S(1)} %copy-done.1, bf16[64,8,8,128]{3,2,1,0:T(8,128)(2,1)S(1)} %copy-done.3), kind=kOutput, calls=%fused_computation.13 | convolution fusion | flops 3224891392 | bytes 14696448 | tf_op jit(solution)/shard_map/while/body/eval_jaxpr/hqk,khd->qhd/dot_general | solution.py:104
  223.2 1.3 fusion.8
  224.5 4.7 %copy.70 = bf16[1,512,1024]{2,0,1:T(2,128)(2,1)S(1)} copy(bf16[1,512,1024]{1,2,0:T(8,128)(2,1)} %bitcast.78) | data formatting | bytes 2097152 | tf_op jit(solution)/shard_map/reshape | solution.py:113
  229.2 0.5 broadcast.156
  229.8 7.8 %reduce.2 = bf16[512,1024]{1,0:T(8,128)(2,1)} reduce(bf16[512,1,1024]{2,1,0:T(2,128)(2,1)S(1)} %bitcast.77, bf16[]{:T(256)} %broadcast.156), dimensions={1}, to_apply=%bitcast.55.reduce_sub_computation | reduce | bytes 2097154
  237.5 2.6 reshape.245
  240.2 3.6 %all-to-all-start.2 = ((bf16[8,2,32768]{2,1,0:T(2,128)(2,1)}), bf16[8,2,32768]{2,1,0:T(2,128)(2,1)S(1)}, u32[]{:S(2)}, u32[]{:S(2)}) async-start(bf16[8,2,32768]{2,1,0:T(2,128)(2,1)} %reshape.245), calls=%async_computation.2 | async-start | bytes 2097152 | tf_op jit(solution)/shard_map/all_to_all | solution.py:114
  243.7 0.1 reshape.217
  243.9 0.2 copy.60
  244.1 0.0 copy-done.6
  244.1 0.1 copy.59
  244.3 26.0 %all-to-all-done.2 = bf16[8,2,32768]{2,1,0:T(2,128)(2,1)S(1)} async-done(((bf16[8,2,32768]{2,1,0:T(2,128)(2,1)}), bf16[8,2,32768]{2,1,0:T(2,128)(2,1)S(1)}, u32[]{:S(2)}, u32[]{:S(2)}) %all-to-all-start.2) | async-done | bytes 1048608 | tf_op jit(solution)/shard_map/all_to_all | solution.py:114
  270.2 3.5 %reshape.246 = bf16[512,1,1024]{2,1,0:T(2,128)(2,1)} reshape(bf16[8,2,32768]{2,1,0:T(2,128)(2,1)S(1)} %all-to-all-done.2) | data formatting | bytes 2097152
  273.7 2.0 copy.94
  275.6 2.1 gather_fusion.2
  277.7 0.4 gather.23
  278.2 5.0 %multiply_reduce_fusion = bf16[256,1024]{1,0:T(8,128)(2,1)} fusion(bf16[256,2,1024]{2,1,0:T(2,128)(2,1)S(1)} %gather.23, pred[256,2]{1,0:T(8,128)(4,1)S(1)} %copy.60, f32[256,2]{1,0:T(8,128)S(1)} %copy.59), kind=kLoop, calls=%fused_computation.15 | loop fusion | flops 1835008 | bytes 1575424 | tf_op jit(solution)/shard_map/reduce_sum | solution.py:119
  (19 shorter events, 0.2 us)
Async XLA Ops:
  6.5 4.1 %copy-start = (bf16[256,2048]{1,0:T(8,128)(2,1)S(1)}, bf16[256,2048]{1,0:T(8,128)(2,1)}, u32[]{:S(2)}) copy-start(bf16[256,2048]{1,0:T(8,128)(2,1)} %param.8) | copy-start | bytes 3145732
  6.5 2.3 copy-start.5
  6.5 62.1 %all-gather.10.cloned.1.call-start = ((), (), s32[]{:S(2)}) async-start(), calls=%async_computation.5 | async-start | bytes 5242880 | tf_op jit(solution)/shard_map/all_gather | solution.py:68
  7.3 111.8 %all-gather.6.cloned.1.call-start = ((), (), s32[]{:S(2)}) async-start(), calls=%async_computation.3 | async-start | bytes 5242880 | tf_op jit(solution)/shard_map/all_gather | solution.py:74
  8.0 165.5 %all-gather.8.cloned.1.call-start = ((), (), s32[]{:S(2)}) async-start(), calls=%async_computation.4 | async-start | bytes 5242880 | tf_op jit(solution)/shard_map/all_gather | solution.py:52
  8.7 193.0 %all-gather.12.cloned.1.call-start = ((), (), s32[]{:S(2)}) async-start(), calls=%async_computation.6 | async-start | bytes 1310720 | tf_op jit(solution)/shard_map/all_gather | solution.py:14
  68.7 1.4 copy-start.4
  124.2 1.0 copy-start.2
  182.1 31.3 %all-to-all-start.1 = ((bf16[8,64,1024]{2,1,0:T(8,128)(2,1)}), bf16[8,64,1024]{2,1,0:T(8,128)(2,1)}, u32[]{:S(2)}, u32[]{:S(2)}) async-start(bf16[8,64,1024]{2,1,0:T(8,128)(2,1)} %select_select_fusion.1), calls=%async_computation.1 | async-start | bytes 2097152 | tf_op jit(solution)/shard_map/all_to_all | solution.py:61
  216.1 1.2 copy-start.1
  216.2 1.5 copy-start.3
  237.5 6.5 %copy-start.6 = (s32[256,2]{0,1:T(2,128)S(1)}, s32[256,2]{0,1:T(2,128)}, u32[]{:S(2)}) copy-start(s32[256,2]{0,1:T(2,128)} %param.10) | copy-start | bytes 6148
  240.2 30.1 %all-to-all-start.2 = ((bf16[8,2,32768]{2,1,0:T(2,128)(2,1)}), bf16[8,2,32768]{2,1,0:T(2,128)(2,1)S(1)}, u32[]{:S(2)}, u32[]{:S(2)}) async-start(bf16[8,2,32768]{2,1,0:T(2,128)(2,1)} %reshape.245), calls=%async_computation.2 | async-start | bytes 2097152 | tf_op jit(solution)/shard_map/all_to_all | solution.py:114
Sparse Core Ops, SparseCore 0:
  9.2 55.3 all-gather.9
  66.4 52.5 all-gather.5
  120.9 52.5 all-gather.7
  175.2 26.4 all-gather.11
where the time goes:
time: 290 us
  waiting for transfers between devices  142 us (49%)
  blocking collectives  55.2 us (19%)
  local copies, waits for them, and re-layouts  28.1 us (10%)
  matrix products  23 us (8%)
  other arithmetic  19.1 us (7%)
  between operations  13.4 us (5%)
  starting transfers between devices  8.28 us (3%)
    all_to_all x1, blocking collectives, on_device(): lax.all_to_all(sent_rows, 'mem', split_axis=0, concat_axis=1, tiled=True)  55.2 us
    all_gather x1, waiting for transfers between devices, on_device(): lax.all_gather(query_weight, 'seq', axis=0, tiled=True)  47.1 us
    all_gather x1, waiting for transfers between devices, on_device(): lax.all_gather(value_weight, 'seq', axis=1, tiled=True)  41.9 us
    all_to_all x1, waiting for transfers between devices, on_device(): lax.all_to_all(normed, 'mem', split_axis=1, concat_axis=0, tiled=True)  26 us
    all_gather x1, waiting for transfers between devices, entering(): gathered = lax.all_gather(array.astype(jnp.bfloat16), axis)  13.9 us
    unnamed x19, local copies, waits for them, and re-layouts  12.9 us
    all_to_all x1, waiting for transfers between devices, on_device(): lax.all_to_all(sent_queries, 'mem', split_axis=0, concat_axis=1, tiled=True)  11.5 us
    unnamed x1, other arithmetic  7.77 us
  transfers between devices with their start and end apart: 6, of which 5 were waited for; matrix products, arithmetic and copies ran while one was open for 10% of the time, Pallas kernels for 0%

commit v1 on v0

--- a/solution.py
+++ b/solution.py
@@ -68,12 +68,38 @@
         lax.all_gather(key_weight, "seq", axis=1, tiled=True),
         preferred_element_type=jnp.float32,
     )
-    value_part = jnp.einsum(
+    peers, mine, rows = (lax.axis_size("seq"), lax.axis_index("seq"), value_weight.shape[1])
+    forward = [(i, (i + 1) % peers) for i in range(peers)]
+    downward = [(i, (i - 1) % peers) for i in range(peers)]
+    middle = peers // 2
+    from_left = from_right = value_weight
+    total = jnp.einsum(
         "mrc,mch->mrh",
-        columns,
-        lax.all_gather(value_weight, "seq", axis=1, tiled=True),
+        lax.dynamic_slice_in_dim(columns, mine * rows, value_weight.shape[1], axis=2),
+        value_weight,
         preferred_element_type=jnp.float32,
     )
+    for lap in range(1, middle + 1):
+        from_left = lax.ppermute(from_left, "seq", forward)
+        if lap < peers - middle:
+            from_right = lax.ppermute(from_right, "seq", downward)
+            total = total + jnp.einsum(
+                "mrc,mch->mrh",
+                lax.dynamic_slice_in_dim(
+                    columns, (mine + lap) % peers * rows, from_right.shape[1], axis=2
+                ),
+                from_right,
+                preferred_element_type=jnp.float32,
+            )
+        total = total + jnp.einsum(
+            "mrc,mch->mrh",
+            lax.dynamic_slice_in_dim(
+                columns, (mine - lap) % peers * rows, from_left.shape[1], axis=2
+            ),
+            from_left,
+            preferred_element_type=jnp.float32,
+        )
+    value_part = total
     keys = key_part
     values = value_part
     keys = keys.astype(jnp.bfloat16)

time: 290 us -> 279 us (0.962)
  blocking collectives: 55.2 us -> 0 us
  waiting for transfers between devices: 142 us -> 173 us
  starting transfers between devices: 8.28 us -> 17.6 us
  matrix products: 23 us -> 27.7 us
    ppermute x0 -> x3, waiting for transfers between devices: none -> 98.7 us  [the longest x2 71.5 us: on_device(): from_left = lax.ppermute(from_left, 'seq', forward)]
    all_to_all x1 -> x0, blocking collectives: 55.2 us -> none  [on_device(): lax.all_to_all(sent_rows, 'mem', split_axis=0, concat_axis=1, tiled=True)]
    all_gather x1 -> x0, waiting for transfers between devices: 41.9 us -> none  [on_device(): lax.all_gather(value_weight, 'seq', axis=1, tiled=True)]
    all_gather x1, waiting for transfers between devices: 47.1 us -> 14.6 us  [on_device(): lax.all_gather(query_weight, 'seq', axis=0, tiled=True)]
    all_to_all x0 -> x1, waiting for transfers between devices: none -> 7.01 us  [on_device(): lax.all_to_all(sent_rows, 'mem', split_axis=0, concat_axis=1, tiled=True)]
    all_to_all x0 -> x1, starting transfers between devices: none -> 6.35 us  [on_device(): lax.all_to_all(sent_rows, 'mem', split_axis=0, concat_axis=1, tiled=True)]
    dot_general x1 -> x4, matrix products: 5.15 us -> 8.89 us  [the longest x2 4.25 us: on_device(): jnp.einsum('mrc,mch->mrh', lax.dynamic_slice_in_dim(columns, (mine - lap)...]
    ppermute x0 -> x3, starting transfers between devices: none -> 2.98 us  [the longest x2 1.55 us: on_device(): from_left = lax.ppermute(from_left, 'seq', forward)]
  transfers between devices with their start and end apart: 6 -> 9, of which waited for: 5 -> 8; matrix products, arithmetic and copies ran while one was open for 10% -> 12% of each run, Pallas kernels for 0% -> 0%
where the time goes in v1:
time: 279 us; the launch traced here: 278 us
  waiting for transfers between devices  173 us (62%)
  matrix products  27.7 us (10%)
  local copies, waits for them, and re-layouts  25.5 us (9%)
  other arithmetic  20.5 us (7%)
  starting transfers between devices  17.6 us (6%)
  between operations  13.4 us (5%)
    ppermute x2, waiting for transfers between devices, on_device(): from_left = lax.ppermute(from_left, 'seq', forward)  71.5 us
    ppermute x1, waiting for transfers between devices, on_device(): from_right = lax.ppermute(from_right, 'seq', downward)  27.2 us
    all_to_all x1, waiting for transfers between devices, on_device(): lax.all_to_all(normed, 'mem', split_axis=1, concat_axis=0, tiled=True)  26 us
    all_gather x1, waiting for transfers between devices, on_device(): lax.all_gather(query_weight, 'seq', axis=0, tiled=True)  14.6 us
    all_gather x1, waiting for transfers between devices, entering(): gathered = lax.all_gather(array.astype(jnp.bfloat16), axis)  14 us
    all_to_all x1, waiting for transfers between devices, on_device(): lax.all_to_all(sent_queries, 'mem', split_axis=0, concat_axis=1, tiled=True)  11.3 us
    unnamed x21, local copies, waits for them, and re-layouts  10.3 us
    unnamed x1, other arithmetic  7.77 us
  transfers between devices with their start and end apart: 9, of which 8 were waited for; matrix products, arithmetic and copies ran while one was open for 12% of the time, Pallas kernels for 0%

profile of v1, /device:TPU:0, one launch (start us, length us, event | category | flops | bytes accessed | tf_op | source)
XLA Modules:
  0.0 277.8 jit_solution(18084477628756653757)
XLA Ops:
  6.5 0.7 all-gather.7.cloned.1.call-update
  7.3 0.0 all-gather.5.cloned.1.call-start
  7.3 0.7 all-gather.5.cloned.1.call-update
  8.0 0.0 copy-done.6
  8.0 0.6 reduce-window.6
  8.6 0.2 slice_reduce_fusion
  8.9 0.1 bitcast_subtract_fusion
  9.0 0.1 copy.61
  9.1 0.1 reshape.236
  9.3 0.2 fusion.24
  9.5 0.2 select_reduce_fusion
  9.7 0.1 reduce_sum.67
  9.8 0.1 broadcast_in_dim.94
  9.9 0.0 copy-done
  9.9 2.5 gather_fusion
  12.3 1.7 select_select_fusion
  14.1 6.4 %all-to-all-start = ((bf16[8,64,2048]{2,1,0:T(8,128)(2,1)}), bf16[8,64,2048]{2,1,0:T(8,128)(2,1)S(1)}, u32[]{:S(2)}, u32[]{:S(2)}) async-start(bf16[8,64,2048]{2,1,0:T(8,128)(2,1)} %select_select_fusion), calls=%async_computation | async-start | bytes 4194304 | tf_op jit(solution)/shard_map/all_to_all | solution.py:60
  20.4 0.0 all-gather.9.cloned.1.call-start
  20.5 1.5 collective-permute-start.1
  22.0 1.4 collective-permute-start
  23.4 39.0 %collective-permute-done.1 = bf16[1,512,1024]{2,1,0:T(8,128)(2,1)} collective-permute-done((bf16[1,512,1024]{2,1,0:T(8,128)(2,1)}, bf16[1,512,1024]{2,1,0:T(8,128)(2,1)}, u32[]{:S(2)}, u32[]{:S(2)}) %collective-permute-start.1) | collective-permute-done | bytes 1048608 | tf_op jit(solution)/shard_map/ppermute | solution.py:83
  62.4 0.0 collective-permute-start.2
  62.4 7.0 %all-to-all-done = bf16[8,64,2048]{2,1,0:T(8,128)(2,1)S(1)} async-done(((bf16[8,64,2048]{2,1,0:T(8,128)(2,1)}), bf16[8,64,2048]{2,1,0:T(8,128)(2,1)S(1)}, u32[]{:S(2)}, u32[]{:S(2)}) %all-to-all-start) | async-done | bytes 2097184 | tf_op jit(solution)/shard_map/all_to_all | solution.py:60
  69.4 2.7 fusion.22
  72.1 2.0 fusion.18
  74.1 27.2 %collective-permute-done = bf16[1,512,1024]{2,1,0:T(8,128)(2,1)} collective-permute-done((bf16[1,512,1024]{2,1,0:T(8,128)(2,1)}, bf16[1,512,1024]{2,1,0:T(8,128)(2,1)}, u32[]{:S(2)}, u32[]{:S(2)}) %collective-permute-start) | collective-permute-done | bytes 1048608 | tf_op jit(solution)/shard_map/ppermute | solution.py:85
  101.3 1.9 fusion.20
  103.2 32.5 %collective-permute-done.2 = bf16[1,512,1024]{2,1,0:T(8,128)(2,1)} collective-permute-done((bf16[1,512,1024]{2,1,0:T(8,128)(2,1)}, bf16[1,512,1024]{2,1,0:T(8,128)(2,1)}, u32[]{:S(2)}, u32[]{:S(2)}) %collective-permute-start.2) | collective-permute-done | bytes 1048608 | tf_op jit(solution)/shard_map/ppermute | solution.py:83
  135.8 2.3 fusion.13
  138.1 0.0 all-gather.7.cloned.1.call-done
  138.1 6.1 %fusion.10 = bf16[512,1024]{1,0:T(8,128)(2,1)} fusion(bf16[512,2048]{1,0:T(8,128)(2,1)} %bitcast.98, bf16[1,2048,1024]{2,1,0:T(8,128)(2,1)} %all-gather.7.cloned.1.call-done), kind=kOutput, calls=%fused_computation.18 | convolution fusion | flops 2148007936 | bytes 7340032 | tf_op jit(solution)/shard_map/mrc,mch->mrh/dot_general | solution.py:65
  144.2 1.5 copy.74
  145.7 1.4 fusion.48
  147.1 0.0 all-gather.9.cloned.1.call-update
  147.1 14.6 %all-gather.5.cloned.1.call-done = bf16[2048,1024]{1,0:T(8,128)(2,1)} async-done(((bf16[512,1024]{1,0:T(8,128)(2,1)}), bf16[2048,1024]{1,0:T(8,128)(2,1)}) %all-gather.5.cloned.1.call-update) | async-done | bytes 4194320 | tf_op jit(solution)/shard_map/all_gather | solution.py:52
  161.7 3.4 %convolution_convert_fusion = bf16[256,1024]{1,0:T(8,128)(2,1)S(1)} fusion(bf16[256,2048]{1,0:T(8,128)(2,1)S(1)} %copy-done, bf16[2048,1024]{1,0:T(8,128)(2,1)} %all-gather.5.cloned.1.call-done), kind=kOutput, calls=%fused_computation.20 | convolution fusion | flops 1074003968 | bytes 5767168 | tf_op jit(solution)/shard_map/dot_general | solution.py:50
  165.1 2.8 %gather_fusion.1 = bf16[512,1024]{1,0:T(8,128)(2,1)} fusion(bf16[256,1024]{1,0:T(8,128)(2,1)S(1)} %convolution_convert_fusion, s32[1024]{0:T(1024)S(1)} %pad_clamp_fusion.1), kind=kCustom, calls=%fused_computation.1 | custom fusion | bytes 2099200 | tf_op jit(solution)/shard_map/jit(_take)/gather | solution.py:56
  167.9 2.4 select_select_fusion.1
  170.4 4.6 %all-to-all-start.1 = ((bf16[8,64,1024]{2,1,0:T(8,128)(2,1)}), bf16[8,64,1024]{2,1,0:T(8,128)(2,1)}, u32[]{:S(2)}, u32[]{:S(2)}) async-start(bf16[8,64,1024]{2,1,0:T(8,128)(2,1)} %select_select_fusion.1), calls=%async_computation.1 | async-start | bytes 2097152 | tf_op jit(solution)/shard_map/all_to_all | solution.py:61
  175.0 1.1 fusion.25
  176.1 14.0 %all-gather.9.cloned.1.call-done = bf16[32,128,128]{2,1,0:T(8,128)(2,1)} async-done(((bf16[8,128,128]{2,1,0:T(8,128)(2,1)}), bf16[32,128,128]{2,1,0:T(8,128)(2,1)}) %all-gather.9.cloned.1.call-update) | async-done | bytes 1048592 | tf_op jit(solution)/shard_map/all_gather | solution.py:14
  190.1 0.2 while.2
  190.3 11.3 %all-to-all-done.1 = bf16[8,64,1024]{2,1,0:T(8,128)(2,1)} async-done(((bf16[8,64,1024]{2,1,0:T(8,128)(2,1)}), bf16[8,64,1024]{2,1,0:T(8,128)(2,1)}, u32[]{:S(2)}, u32[]{:S(2)}) %all-to-all-start.1) | async-done | bytes 1048608 | tf_op jit(solution)/shard_map/all_to_all | solution.py:61
  201.6 1.6 copy.76
  203.2 0.0 copy-start.5
  203.2 1.2 fusion.30
  204.5 1.1 fusion.28
  205.6 0.1 copy-done.4
  205.7 5.5 %fusion.5 = (f32[512,8]{0,1:T(8,128)S(1)}, f32[8,128,512]{2,1,0:T(8,128)S(1)}) fusion(f32[8,128,512]{2,1,0:T(8,128)S(1)} %fusion.28, f32[8,512,512]{2,1,0:T(8,128)S(1)} %fusion.30, f32[512,512]{1,0:T(8,128)S(1)} %copy-done.4, bf16[64,8,8,128]{3,2,1,0:T(8,128)(2,1)S(1)} %fusion.13), kind=kOutput, calls=%fused_computation.11 | convolution fusion | flops 3224891392 | bytes 14696448 | tf_op jit(solution)/shard_map/while/body/eval_jaxpr/hqk,khd->qhd/dot_general | solution.py:130
  211.3 1.3 fusion.6
  212.6 4.7 %copy.70 = bf16[1,512,1024]{2,0,1:T(2,128)(2,1)S(1)} copy(bf16[1,512,1024]{1,2,0:T(8,128)(2,1)} %bitcast.100) | data formatting | bytes 2097152 | tf_op jit(solution)/shard_map/reshape | solution.py:139
  217.3 0.5 broadcast.163
  217.8 7.8 %reduce.2 = bf16[512,1024]{1,0:T(8,128)(2,1)} reduce(bf16[512,1,1024]{2,1,0:T(2,128)(2,1)S(1)} %bitcast.99, bf16[]{:T(256)} %broadcast.163), dimensions={1}, to_apply=%bitcast.73.reduce_sub_computation | reduce | bytes 2097154
  225.6 2.6 reshape.277
  228.2 3.6 %all-to-all-start.2 = ((bf16[8,2,32768]{2,1,0:T(2,128)(2,1)}), bf16[8,2,32768]{2,1,0:T(2,128)(2,1)S(1)}, u32[]{:S(2)}, u32[]{:S(2)}) async-start(bf16[8,2,32768]{2,1,0:T(2,128)(2,1)} %reshape.277), calls=%async_computation.2 | async-start | bytes 2097152 | tf_op jit(solution)/shard_map/all_to_all | solution.py:140
  231.8 0.1 reshape.249
  231.9 0.2 copy.60
  232.2 0.1 copy.59
  232.3 26.0 %all-to-all-done.2 = bf16[8,2,32768]{2,1,0:T(2,128)(2,1)S(1)} async-done(((bf16[8,2,32768]{2,1,0:T(2,128)(2,1)}), bf16[8,2,32768]{2,1,0:T(2,128)(2,1)S(1)}, u32[]{:S(2)}, u32[]{:S(2)}) %all-to-all-start.2) | async-done | bytes 1048608 | tf_op jit(solution)/shard_map/all_to_all | solution.py:140
  258.3 3.5 %reshape.278 = bf16[512,1,1024]{2,1,0:T(2,128)(2,1)} reshape(bf16[8,2,32768]{2,1,0:T(2,128)(2,1)S(1)} %all-to-all-done.2) | data formatting | bytes 2097152
  261.7 2.0 copy.94
  263.7 2.1 gather_fusion.2
  265.8 0.4 gather.23
  266.2 5.0 %multiply_reduce_fusion = bf16[256,1024]{1,0:T(8,128)(2,1)} fusion(bf16[256,2,1024]{2,1,0:T(2,128)(2,1)S(1)} %gather.23, pred[256,2]{1,0:T(8,128)(4,1)S(1)} %copy.60, f32[256,2]{1,0:T(8,128)S(1)} %copy.59), kind=kLoop, calls=%fused_computation.13 | loop fusion | flops 1835008 | bytes 1575424 | tf_op jit(solution)/shard_map/reduce_sum | solution.py:145
  (28 shorter events, 0.2 us)
Async XLA Ops:
  6.5 3.3 %copy-start = (bf16[256,2048]{1,0:T(8,128)(2,1)S(1)}, bf16[256,2048]{1,0:T(8,128)(2,1)}, u32[]{:S(2)}) copy-start(bf16[256,2048]{1,0:T(8,128)(2,1)} %param.8) | copy-start | bytes 3145732
  6.5 1.5 copy-start.6
  6.5 131.5 %all-gather.7.cloned.1.call-start = ((), (), s32[]{:S(2)}) async-start(), calls=%async_computation.4 | async-start | bytes 5242880 | tf_op jit(solution)/shard_map/all_gather | solution.py:68
  7.3 154.4 %all-gather.5.cloned.1.call-start = ((), (), s32[]{:S(2)}) async-start(), calls=%async_computation.3 | async-start | bytes 5242880 | tf_op jit(solution)/shard_map/all_gather | solution.py:52
  14.1 55.4 %all-to-all-start = ((bf16[8,64,2048]{2,1,0:T(8,128)(2,1)}), bf16[8,64,2048]{2,1,0:T(8,128)(2,1)S(1)}, u32[]{:S(2)}, u32[]{:S(2)}) async-start(bf16[8,64,2048]{2,1,0:T(8,128)(2,1)} %select_select_fusion), calls=%async_computation | async-start | bytes 4194304 | tf_op jit(solution)/shard_map/all_to_all | solution.py:60
  20.4 169.7 %all-gather.9.cloned.1.call-start = ((), (), s32[]{:S(2)}) async-start(), calls=%async_computation.5 | async-start | bytes 1310720 | tf_op jit(solution)/shard_map/all_gather | solution.py:14
  20.5 42.0 %collective-permute-start.1 = (bf16[1,512,1024]{2,1,0:T(8,128)(2,1)}, bf16[1,512,1024]{2,1,0:T(8,128)(2,1)}, u32[]{:S(2)}, u32[]{:S(2)}) collective-permute-start(bf16[1,512,1024]{2,1,0:T(8,128)(2,1)} %param.13), channel_id=1, source_target_pairs={{0,8},{8,16},{16,24},{24,0},{1,9},{9,17},{17,25},{25,1},{2,10},{10... | collective-permute-start | bytes 3145736 | tf_op jit(solution)/shard_map/ppermute | solution.py:83
  22.0 79.3 %collective-permute-start = (bf16[1,512,1024]{2,1,0:T(8,128)(2,1)}, bf16[1,512,1024]{2,1,0:T(8,128)(2,1)}, u32[]{:S(2)}, u32[]{:S(2)}) collective-permute-start(bf16[1,512,1024]{2,1,0:T(8,128)(2,1)} %param.13), channel_id=1, source_target_pairs={{0,24},{8,0},{16,8},{24,16},{1,25},{9,1},{17,9},{25,17},{2,26},{10... | collective-permute-start | bytes 3145736 | tf_op jit(solution)/shard_map/ppermute | solution.py:85
  62.4 73.3 %collective-permute-start.2 = (bf16[1,512,1024]{2,1,0:T(8,128)(2,1)}, bf16[1,512,1024]{2,1,0:T(8,128)(2,1)}, u32[]{:S(2)}, u32[]{:S(2)}) collective-permute-start(bf16[1,512,1024]{2,1,0:T(8,128)(2,1)} %collective-permute-done.1), channel_id=1, source_target_pairs={{0,8},{8,16},{16,24},{24,0},{1,9},{9,17},{17,25},{25,1},{2,10},{10... | collective-permute-start | bytes 3145736 | tf_op jit(solution)/shard_map/ppermute | solution.py:83
  69.4 31.8 %copy-start.3 = (bf16[8,64,2048]{2,1,0:T(8,128)(2,1)}, bf16[8,64,2048]{2,1,0:T(8,128)(2,1)S(1)}, u32[]{:S(2)}) copy-start(bf16[8,64,2048]{2,1,0:T(8,128)(2,1)S(1)} %all-to-all-done) | copy-start | bytes 6291460
  145.7 1.4 copy-start.1
  170.4 31.3 %all-to-all-start.1 = ((bf16[8,64,1024]{2,1,0:T(8,128)(2,1)}), bf16[8,64,1024]{2,1,0:T(8,128)(2,1)}, u32[]{:S(2)}, u32[]{:S(2)}) async-start(bf16[8,64,1024]{2,1,0:T(8,128)(2,1)} %select_select_fusion.1), calls=%async_computation.1 | async-start | bytes 2097152 | tf_op jit(solution)/shard_map/all_to_all | solution.py:61
  201.6 1.6 copy-start.2
  203.2 1.3 copy-start.5
  204.5 1.2 copy-start.4
  225.6 6.5 %copy-start.7 = (s32[256,2]{0,1:T(2,128)S(1)}, s32[256,2]{0,1:T(2,128)}, u32[]{:S(2)}) copy-start(s32[256,2]{0,1:T(2,128)} %param.10) | copy-start | bytes 6148
  228.2 30.1 %all-to-all-start.2 = ((bf16[8,2,32768]{2,1,0:T(2,128)(2,1)}), bf16[8,2,32768]{2,1,0:T(2,128)(2,1)S(1)}, u32[]{:S(2)}, u32[]{:S(2)}) async-start(bf16[8,2,32768]{2,1,0:T(2,128)(2,1)} %reshape.277), calls=%async_computation.2 | async-start | bytes 2097152 | tf_op jit(solution)/shard_map/all_to_all | solution.py:140
Sparse Core Ops, SparseCore 0:
  9.2 87.1 all-gather.6
  98.3 63.3 all-gather.4
  163.5 26.4 all-gather.8
